TPU v7x, 1024 devices: a whole 8x8x8 slice. The times are simulated.
1024 devices in a mesh: dp: 32 (over y, x_lo), expert: 32 (over z, x_hi, core).
Axes of the slice: x: 8 (x_hi: 2, x_lo: 4; x = x_hi * 4 + x_lo), y: 8, z: 8, core: 2. Of those that a mesh axis runs over, the one named last changes fastest.
Arguments:
- shortcut_in: bfloat16 [512, 7168], P('expert', 'dp'), may hold values from -6 to 6
- current_in: bfloat16 [512, 7168], P('expert', 'dp'), may hold values from -6 to 6
- expert_ids: int32 [512, 8], P('expert'), may hold values from 0 to 31, all different within a row; in each aligned block of 16 rows (0 to 15, 16 to 31, ...) at most 6 rows name the same one
- route_weight: float32 [512, 8], P('expert'), may hold values from 0.1 to 1
- gate_weight: bfloat16 [32, 7168, 2048], P('expert', 'dp'), may hold values from -0.125 to 0.125
- up_weight: bfloat16 [32, 7168, 2048], P('expert', 'dp'), may hold values from -0.125 to 0.125
- down_weight: bfloat16 [32, 2048, 7168], P('expert', None, 'dp'), may hold values from -0.125 to 0.125
- shared_gate: bfloat16 [7168, 2048], P('dp'), may hold values from -0.125 to 0.125
- shared_up: bfloat16 [7168, 2048], P('dp'), may hold values from -0.125 to 0.125
- shared_down: bfloat16 [2048, 7168], P(None, 'dp'), may hold values from -0.125 to 0.125
Outputs:
- mixed: bfloat16 [512, 7168], P('expert', 'dp')
Inputs may be any that keep to these rules, and one draw needn't show every extreme that they name: `expert_ids`: each row names 8 different experts. In each aligned block of 16 rows (the tokens of one index of the expert axis) no expert is named by more than 6 rows, and in at least one such block some expert is named by exactly 6 rows.
All inputs are finite; a program needn't handle non-finite values.
Results may differ from a plain program's by a relative error of at most 0.035.
Values may be sent and summed in bfloat16 or wider, within the bound.
No kernel may reach another device: no remote copies, remote signals or barrier semaphores. Data moves between devices by JAX's collectives and lax.ppermute only.
A program may use at most 32 MiB of HBM per device.

v0:
```python
import jax
import jax.numpy as jnp
from jax import lax
from jax.sharding import PartitionSpec as P


def in_blocks(array, dim, length):
    dims = array.shape
    tiles = array.reshape(*dims[:dim], length, dims[dim] // length, *dims[dim + 1 :])
    return jnp.moveaxis(tiles, dim, 0)


def summed_on_arrival(array, axis, dim):
    length = lax.axis_size(axis)
    tiles = lax.all_to_all(in_blocks(array, dim, length), axis, 0, 0, tiled=True)
    return jnp.sum(tiles.astype(jnp.float32), axis=0)


def laid_out(tiles, dim):
    dims = list(tiles.shape[1:])
    dims[dim] *= tiles.shape[0]
    return jnp.moveaxis(tiles, 0, dim).reshape(dims)


def copy_for_each(array, axis):
    copies = jnp.broadcast_to(array, (lax.axis_size(axis), *array.shape))
    return lax.all_to_all(copies, axis, split_axis=0, concat_axis=0, tiled=True)


def gathered_copies(array, axis, dim):
    return laid_out(copy_for_each(array, axis), dim)


def activate(summed):
    return (jax.nn.silu(summed[:, 0]) * summed[:, 1]).astype(jnp.bfloat16)


def hidden_of(partial_value):
    groups = lax.axis_size("dp")
    length = partial_value.shape[0]
    extra = (groups - length % groups) % groups
    padded = jnp.concatenate(
        [partial_value, jnp.zeros((extra,) + partial_value.shape[1:], partial_value.dtype)], axis=0
    )
    summed = summed_on_arrival(padded.astype(jnp.bfloat16), "dp", 0)
    gathered = gathered_copies(activate(summed), "dp", 0)
    return gathered[:length]


def send_rows(outgoing):
    return lax.all_to_all(outgoing, "expert", split_axis=0, concat_axis=0, tiled=True)


def expert_partial(arrived, gate_weight, up_weight):
    gate = jnp.einsum("sacd,adh->sach", arrived, gate_weight, preferred_element_type=jnp.float32)
    upper = jnp.einsum("sacd,adh->sach", arrived, up_weight, preferred_element_type=jnp.float32)
    stacked = jnp.stack([gate, upper], axis=3)
    return stacked.reshape(-1, 2, gate_weight.shape[2])


def local(
    shortcut_in,
    current_in,
    expert_ids,
    route_weight,
    gate_weight,
    up_weight,
    down_weight,
    shared_gate,
    shared_up,
    shared_down,
):
    sources = lax.axis_size("expert")
    local_experts = gate_weight.shape[0]
    experts = sources * local_experts
    tokens, top = expert_ids.shape
    capacity = 3 * tokens * top // (2 * experts)
    width = shortcut_in.shape[1]
    hidden_units = gate_weight.shape[2]
    flat_ids = expert_ids.reshape(-1)
    onehot = (flat_ids[:, None] == jnp.arange(experts, dtype=jnp.int32)[None, :]).astype(jnp.int32)
    rank = jnp.sum((jnp.cumsum(onehot, axis=0) - 1) * onehot, axis=1)
    slot = (flat_ids * capacity + rank).reshape(tokens, top)
    positions = jnp.arange(experts * capacity, dtype=jnp.int32)
    place = jnp.sum((slot[None, :, :] == positions[:, None, None]).astype(jnp.bfloat16), axis=2)
    outgoing = jnp.dot(place, shortcut_in, preferred_element_type=jnp.float32).astype(jnp.bfloat16)
    outgoing = outgoing.reshape(sources, local_experts * capacity, width)
    shared_gate_sum = jnp.dot(current_in, shared_gate, preferred_element_type=jnp.float32)
    shared_up_sum = jnp.dot(current_in, shared_up, preferred_element_type=jnp.float32)
    shared_partial = jnp.stack([shared_gate_sum, shared_up_sum], axis=1)
    routed_rows = experts * capacity
    arrived = send_rows(outgoing).reshape(sources, local_experts, capacity, width)
    routed_partial = expert_partial(arrived, gate_weight, up_weight)
    joined = hidden_of(jnp.concatenate([routed_partial, shared_partial], axis=0))
    routed_hidden = joined[:routed_rows]
    shared_hidden = joined[routed_rows:]
    routed_hidden = routed_hidden.reshape(sources, local_experts, capacity, hidden_units)
    expert_out = jnp.einsum(
        "sach,ahd->sacd", routed_hidden, down_weight, preferred_element_type=jnp.float32
    ).astype(jnp.bfloat16)
    returned = lax.all_to_all(
        expert_out.reshape(sources, local_experts * capacity, width),
        "expert",
        split_axis=0,
        concat_axis=0,
        tiled=True,
    )
    picked = returned.reshape(routed_rows, width)[slot]
    routed = jnp.sum(route_weight[:, :, None] * picked.astype(jnp.float32), axis=1)
    shared_out = jnp.dot(shared_hidden, shared_down, preferred_element_type=jnp.float32)
    return (shared_out + routed).astype(jnp.bfloat16)


def solution(mesh):
    placed = (
        P("expert", "dp"),
        P("expert", "dp"),
        P("expert", None),
        P("expert", None),
        P("expert", "dp", None),
        P("expert", "dp", None),
        P("expert", None, "dp"),
        P("dp", None),
        P("dp", None),
        P(None, "dp"),
    )
    return jax.shard_map(
        local, mesh=mesh, in_specs=placed, out_specs=P("expert", "dp"), check_vma=False
    )
```

profile of v0, /device:TPU:1, one launch (start us, length us, event | category | flops | bytes accessed | tf_op | source)
XLA Modules:
  0.0 157.9 jit_solution(1276487550852875220)
XLA Ops:
  0.0 0.9 copy.45
  1.1 0.2 reduce_window_sum.11
  1.3 0.2 select_reduce_fusion
  1.5 0.1 fusion.13
  1.7 0.9 convolution_convert_fusion.5
  2.6 0.7 reshape.56
  3.3 23.2 %all-to-all-start = ((bf16[32,6,224]{2,1,0:T(8,128)(2,1)}), bf16[32,6,224]{2,1,0:T(8,128)(2,1)S(1)}, u32[]{:S(2)}, u32[]{:S(2)}) async-start(bf16[32,6,224]{2,1,0:T(8,128)(2,1)} %reshape.56), calls=%async_computation | async-start | bytes 262144 | tf_op jit(solution)/shard_map/all_to_all | solution.py:51
  26.5 2.1 %fusion.2 = bf16[16,1,2048]{2,0,1:T(8,128)(2,1)} fusion(bf16[16,224]{1,0:T(8,128)(2,1)} %param.11, bf16[224,2048]{1,0:T(8,128)(2,1)} %param.17), kind=kOutput, calls=%fused_computation.8 | convolution fusion | flops 14712832 | bytes 990208 | tf_op jit(solution)/shard_map/dot_general | solution.py:88
  28.7 0.9 fusion.3
  29.5 9.4 %all-to-all-done = bf16[32,6,224]{2,1,0:T(8,128)(2,1)S(1)} async-done(((bf16[32,6,224]{2,1,0:T(8,128)(2,1)}), bf16[32,6,224]{2,1,0:T(8,128)(2,1)S(1)}, u32[]{:S(2)}, u32[]{:S(2)}) %all-to-all-start) | async-done | bytes 86048 | tf_op jit(solution)/shard_map/all_to_all | solution.py:51
  38.9 0.4 fusion
  39.3 0.4 copy.48
  39.7 0.3 stack.21
  40.0 1.6 fusion.1
  41.5 0.4 copy.50
  42.0 0.3 stack.22
  42.2 1.4 maximum_maximum_fusion
  43.7 1.9 %copy.51 = bf16[224,2,2048]{2,1,0:T(2,128)(2,1)S(1)} copy(bf16[224,2,2048]{2,0,1:T(8,128)(2,1)S(1)} %maximum_maximum_fusion) | data formatting | bytes 3670016 | tf_op jit(solution)/shard_map/concatenate | solution.py:42
  45.6 51.8 %all_to_all.20 = bf16[32,7,2,2048]{3,2,1,0:T(2,128)(2,1)S(1)} all-to-all(bf16[32,7,2,2048]{3,2,1,0:T(2,128)(2,1)S(1)} %bitcast.65), channel_id=1, replica_groups=mesh['dp'=32,'expert'=32] {'dp'}, dimensions={0} | all-to-all | bytes 3670016 | tf_op jit(solution)/shard_map/all_to_all | solution.py:15
  97.4 1.5 convert_reduce_fusion
  98.9 0.1 fusion.23
  99.0 0.1 broadcast_in_dim.13
  99.1 33.9 %all_to_all.21 = bf16[32,7,2048]{2,1,0:T(8,128)(2,1)S(1)} all-to-all(bf16[32,7,2048]{2,1,0:T(8,128)(2,1)S(1)} %broadcast_in_dim.13), channel_id=1, replica_groups=mesh['dp'=32,'expert'=32] {'dp'}, dimensions={0} | all-to-all | bytes 1835008 | tf_op jit(solution)/shard_map/all_to_all | solution.py:27
  133.0 0.3 reshape.59
  133.4 1.2 reshape.60
  134.6 2.3 %convolution_convert_fusion.4 = bf16[32,6,224]{2,0,1:T(8,128)(2,1)S(1)} fusion(bf16[1,2048,224]{1,2,0:T(8,128)(2,1)} %param.16, bf16[32,6,2048]{2,1,0:T(8,128)(2,1)} %reshape.60), kind=kOutput, calls=%fused_computation.11 | convolution fusion | flops 176203776 | bytes 1789952 | tf_op jit(solution)/shard_map/sach,ahd->sacd/dot_general | solution.py:98
  136.9 0.7 copy.55
  137.6 5.6 %all-to-all-start.3 = ((bf16[32,6,224]{2,1,0:T(8,128)(2,1)}), bf16[32,6,224]{2,1,0:T(8,128)(2,1)S(1)}, u32[]{:S(2)}, u32[]{:S(2)}) async-start(bf16[32,6,224]{2,1,0:T(8,128)(2,1)} %copy.55), calls=%async_computation.3 | async-start | bytes 262144 | tf_op jit(solution)/shard_map/all_to_all | solution.py:101
  143.4 12.5 %all-to-all-done.3 = bf16[32,6,224]{2,1,0:T(8,128)(2,1)S(1)} async-done(((bf16[32,6,224]{2,1,0:T(8,128)(2,1)}), bf16[32,6,224]{2,1,0:T(8,128)(2,1)S(1)}, u32[]{:S(2)}, u32[]{:S(2)}) %all-to-all-start.3) | async-done | bytes 86048 | tf_op jit(solution)/shard_map/all_to_all | solution.py:101
  155.9 0.8 gather_fusion
  156.8 0.1 fusion.9
  156.9 1.0 fusion.4
  (22 shorter events, 0.7 us)
Async XLA Ops:
  0.0 38.9 %copy-start = (bf16[1,224,2048]{2,1,0:T(8,128)(2,1)S(1)}, bf16[1,224,2048]{2,1,0:T(8,128)(2,1)}, u32[]{:S(2)}) copy-start(bf16[1,224,2048]{2,1,0:T(8,128)(2,1)} %param.14) | copy-start | bytes 2752516
  0.0 28.7 %copy-start.3 = (bf16[16,224]{1,0:T(8,128)(2,1)S(1)}, bf16[16,224]{1,0:T(8,128)(2,1)}, u32[]{:S(2)}) copy-start(bf16[16,224]{1,0:T(8,128)(2,1)} %param.11) | copy-start | bytes 21508
  0.0 28.7 %copy-start.1 = (bf16[224,2048]{1,0:T(8,128)(2,1)S(1)}, bf16[224,2048]{1,0:T(8,128)(2,1)}, u32[]{:S(2)}) copy-start(bf16[224,2048]{1,0:T(8,128)(2,1)} %param.18) | copy-start | bytes 2752516
  3.3 35.6 %all-to-all-start = ((bf16[32,6,224]{2,1,0:T(8,128)(2,1)}), bf16[32,6,224]{2,1,0:T(8,128)(2,1)S(1)}, u32[]{:S(2)}, u32[]{:S(2)}) async-start(bf16[32,6,224]{2,1,0:T(8,128)(2,1)} %reshape.56), calls=%async_computation | async-start | bytes 262144 | tf_op jit(solution)/shard_map/all_to_all | solution.py:51
  133.4 9.9 %copy-start.4 = (f32[16,8]{0,1:T(8,128)S(1)}, f32[16,8]{0,1:T(8,128)}, u32[]{:S(2)}) copy-start(f32[16,8]{0,1:T(8,128)} %param.13) | copy-start | bytes 1540
  134.6 22.3 %copy-start.2 = (bf16[2048,224]{0,1:T(8,128)(2,1)S(1)}, bf16[2048,224]{0,1:T(8,128)(2,1)}, u32[]{:S(2)}) copy-start(bf16[2048,224]{0,1:T(8,128)(2,1)} %param.19) | copy-start | bytes 2752516
  137.6 18.2 %all-to-all-start.3 = ((bf16[32,6,224]{2,1,0:T(8,128)(2,1)}), bf16[32,6,224]{2,1,0:T(8,128)(2,1)S(1)}, u32[]{:S(2)}, u32[]{:S(2)}) async-start(bf16[32,6,224]{2,1,0:T(8,128)(2,1)} %copy.55), calls=%async_computation.3 | async-start | bytes 262144 | tf_op jit(solution)/shard_map/all_to_all | solution.py:101
where the time goes:
time: 159 us; the launch traced here: 158 us
  blocking collectives  85.7 us (54%)
  starting transfers between devices  28.8 us (18%)
  waiting for transfers between devices  21.8 us (14%)
  matrix products  8.99 us (6%)
  local copies, waits for them, and re-layouts  8.73 us (5%)
  other arithmetic  3.64 us (2%)
    all_to_all x1, blocking collectives, summed_on_arrival(): lax.all_to_all(in_blocks(array, dim, length), axis, 0, 0, tiled=True)  51.8 us
    all_to_all x1, blocking collectives, copy_for_each(): return lax.all_to_all(copies, axis, split_axis=0, concat_axis=0, tiled=True)  33.9 us
    all_to_all x1, starting transfers between devices, send_rows(): lax.all_to_all(outgoing, 'expert', split_axis=0, concat_axis=0, tiled=True)  23.2 us
    all_to_all x1, waiting for transfers between devices, local(): lax.all_to_all(expert_out.reshape(sources, local_experts * capacity, widt...  12.5 us
    all_to_all x1, waiting for transfers between devices, send_rows(): lax.all_to_all(outgoing, 'expert', split_axis=0, concat_axis=0, tiled=True)  9.35 us
    all_to_all x1, starting transfers between devices, local(): lax.all_to_all(expert_out.reshape(sources, local_experts * capacity, widt...  5.55 us
  transfers between devices with their start and end apart: 2, of which 2 were waited for; matrix products, arithmetic and copies ran while one was open for 2% of the time, Pallas kernels for 0%

commit v1 on v0

v1 whole, which is shorter than its diff:
```python
import jax
import jax.numpy as jnp
from jax import lax
from jax.experimental import pallas as pl
from jax.experimental.pallas import tpu as pltpu
from jax.sharding import PartitionSpec as P

F32 = jnp.float32
BF16 = jnp.bfloat16
LANES = 128
SUB = 8
WIDE = 256


def iota(shape, dim):
    return lax.broadcasted_iota(jnp.int32, shape, dim)


def dot(a, b, dims=((1,), (0,)), precision=None):
    return lax.dot_general(a, b, (dims, ((), ())), precision=precision, preferred_element_type=F32)


def pick_rows(rows, padded, cap):
    r = iota((rows, padded), 0)
    p = iota((rows, padded), 1)
    low = p & (SUB - 1)
    hit = (r == cap * (p >> 3) + low) & (low < cap)
    return jnp.where(hit, 1.0, 0.0).astype(BF16)


def pack_body(cap, ids, weight, routed_in, shared_in, out, mix, wide_r, wide_s):
    top, tokens = ids.shape
    experts = out.shape[0] // SUB
    width = routed_in.shape[1]
    ident = ids[...]
    scale = weight[...]
    e_of = iota((experts, tokens), 0)
    named = jnp.zeros((experts, tokens), F32)
    gains = jnp.zeros((experts, tokens), F32)
    for k in range(top):
        same = e_of == ident[k : k + 1, :]
        named = named + jnp.where(same, 1.0, 0.0)
        gains = gains + jnp.where(same, scale[k : k + 1, :], 0.0)
    row = iota((tokens, tokens), 0)
    col = iota((tokens, tokens), 1)
    rank = dot(named, jnp.where(row < col, 1.0, 0.0))
    count = dot(named, jnp.ones((tokens, tokens), F32))
    free = cap - count
    row = iota((experts, experts), 0)
    col = iota((experts, experts), 1)
    before = dot(jnp.where(col < row, 1.0, 0.0), free)
    tok = iota((experts, tokens), 1).astype(F32) - before
    fits = (tok >= 0.0) & (tok < free)
    slot_r = jnp.where(named > 0.0, rank, -1.0)
    slot_s = jnp.where(fits, count + tok, -1.0)

    def spread(a):
        a = jnp.broadcast_to(a[:, None, :], (experts, SUB, tokens))
        return a.reshape(experts * SUB, tokens)

    place = (iota((experts * SUB, tokens), 0) & (SUB - 1)).astype(F32)
    put_r = spread(slot_r) == place
    put_s = jnp.where(spread(slot_s) == place, 1.0, 0.0)
    mix[...] = jnp.where(put_r, spread(gains), put_s)
    wide_r[...] = jnp.zeros_like(wide_r)
    wide_s[...] = jnp.ones_like(wide_s)
    wide_r[:, :width] = routed_in[...]
    wide_s[:, :width] = shared_in[...]
    sent = dot(jnp.where(put_r, 1.0, 0.0).astype(BF16), wide_r[...])
    sent = sent + dot(put_s.astype(BF16), wide_s[...])
    out[...] = sent.astype(BF16)


def up_body(cap, arrived, gate_w, up_w, shared_gate, shared_up, out, left, right):
    padded, wide = arrived.shape
    width, units = gate_w.shape
    rows = padded // SUB * cap
    half = rows // 2
    compact = dot(pick_rows(rows, padded, cap), arrived[...])
    shared = compact[:, width : width + 1] > 0.5
    left[...] = jnp.where(shared, 0.0, compact).astype(BF16)[:, :width]
    right[...] = jnp.where(shared, compact, 0.0).astype(BF16)[:, :width]
    step = 2 * LANES
    for c in range(units // step):
        cols = slice(c * step, (c + 1) * step)
        for which, (w, s) in enumerate(((gate_w, shared_gate), (up_w, shared_up))):
            value = dot(left[...], w[:, cols]) + dot(right[...], s[:, cols])
            value = value.astype(BF16)
            for b in range(2):
                for j in range(2):
                    owner = 2 * (2 * c + b) + j
                    out[owner, which * half : (which + 1) * half, :] = value[
                        j * half : (j + 1) * half, b * LANES : (b + 1) * LANES
                    ]


def act_body(parts, out):
    sources, both, _ = parts.shape
    half = both // 2
    gate = jnp.zeros((half, LANES), F32)
    upper = jnp.zeros((half, LANES), F32)
    for s in range(sources):
        gate = gate + parts[s, :half, :].astype(F32)
        upper = upper + parts[s, half:, :].astype(F32)
    hidden = (jax.nn.silu(gate) * upper).astype(BF16)
    for s in range(sources):
        out[s] = hidden


def down_body(cap, hidden, arrived, down_t, shared_down_t, out, joined):
    owners, half, _ = hidden.shape
    padded = arrived.shape[0]
    width = down_t.shape[0]
    rows = 2 * half
    for owner in range(owners):
        i, j = owner // 2, owner % 2
        joined[j * half : (j + 1) * half, i * LANES : (i + 1) * LANES] = hidden[owner]
    last = ((1,), (1,))
    own = dot(joined[...], down_t[...], last).astype(BF16)
    common = dot(joined[...], shared_down_t[...], last).astype(BF16)
    back = pick_rows(rows, padded, cap)
    first = ((0,), (0,))
    own = dot(back, own, first)
    common = dot(back, common, first)
    shared = arrived[:, width:].astype(F32)[:, :1] > 0.5
    out[...] = jnp.where(shared, common, own).astype(BF16)


def mix_body(returned, mix, out):
    value = dot(mix[...], returned[...].astype(F32), ((0,), (0,)), lax.Precision.HIGHEST)
    out[...] = value.astype(BF16)


def call(body, shape, dtype, *args, scratch=()):
    single = isinstance(dtype, tuple)
    outs = [jax.ShapeDtypeStruct(s, d) for s, d in zip(shape, dtype)] if single else jax.ShapeDtypeStruct(shape, dtype)
    return pl.pallas_call(body, out_shape=outs, scratch_shapes=list(scratch))(*args)


def local(
    shortcut_in,
    current_in,
    expert_ids,
    route_weight,
    gate_weight,
    up_weight,
    down_weight,
    shared_gate,
    shared_up,
    shared_down,
):
    sources = lax.axis_size("expert")
    owners = lax.axis_size("dp")
    tokens, top = expert_ids.shape
    cap = 3 * tokens * top // (2 * sources)
    width = shortcut_in.shape[1]
    units = gate_weight.shape[2]
    padded = sources * SUB
    rows = sources * cap
    sent, mix = call(
        lambda *r: pack_body(cap, *r),
        ((padded, WIDE), (padded, tokens)),
        (BF16, F32),
        expert_ids.T,
        route_weight.T,
        shortcut_in,
        current_in,
        scratch=(pltpu.VMEM((tokens, WIDE), BF16), pltpu.VMEM((tokens, WIDE), BF16)),
    )
    arrived = lax.all_to_all(sent.reshape(sources, SUB, WIDE), "expert", 0, 0, tiled=True)
    arrived = arrived.reshape(padded, WIDE)
    parts = call(
        lambda *r: up_body(cap, *r),
        (owners, rows, LANES),
        BF16,
        arrived,
        gate_weight[0],
        up_weight[0],
        shared_gate,
        shared_up,
        scratch=(pltpu.VMEM((rows, width), BF16), pltpu.VMEM((rows, width), BF16)),
    )
    parts = lax.all_to_all(parts, "dp", 0, 0, tiled=True)
    copies = call(act_body, (owners, rows // 2, LANES), BF16, parts)
    hidden = lax.all_to_all(copies, "dp", 0, 0, tiled=True)
    results = call(
        lambda *r: down_body(cap, *r),
        (padded, width),
        BF16,
        hidden,
        arrived,
        down_weight[0].T,
        shared_down.T,
        scratch=(pltpu.VMEM((rows, units), BF16),),
    )
    returned = lax.all_to_all(results.reshape(sources, SUB, width), "expert", 0, 0, tiled=True)
    return call(mix_body, (tokens, width), BF16, returned.reshape(padded, width), mix)


def solution(mesh):
    placed = (
        P("expert", "dp"),
        P("expert", "dp"),
        P("expert", None),
        P("expert", None),
        P("expert", "dp", None),
        P("expert", "dp", None),
        P("expert", None, "dp"),
        P("dp", None),
        P("dp", None),
        P(None, "dp"),
    )
    return jax.shard_map(
        local, mesh=mesh, in_specs=placed, out_specs=P("expert", "dp"), check_vma=False
    )
```

time: 159 us -> 145 us (0.912)
  blocking collectives: 85.7 us -> 130 us
  starting transfers between devices: 28.8 us -> 0 us
  waiting for transfers between devices: 21.8 us -> 0 us
  Pallas kernels: 0 us -> 14 us
  matrix products: 8.99 us -> 0 us
  local copies, waits for them, and re-layouts: 8.73 us -> 0 us
  other arithmetic: 3.64 us -> 0 us
    all_to_all x2 -> x4, blocking collectives: 85.7 us -> 130 us  [the longest x1 47.6 us: local(): parts = lax.all_to_all(parts, 'dp', 0, 0, tiled=True)]
    all_to_all x2 -> x0, starting transfers between devices: 28.8 us -> none  [the longest x1 23.2 us: send_rows(): lax.all_to_all(outgoing, 'expert', split_axis=0, concat_axis=0, tiled=True)]
    all_to_all x2 -> x0, waiting for transfers between devices: 21.8 us -> none  [the longest x1 12.5 us: local(): lax.all_to_all(expert_out.reshape(sources, local_experts * capacity, widt...]
    pallas_call x0 -> x5, Pallas kernels: none -> 14 us  [call(): pl.pallas_call(body, out_shape=outs, scratch_shapes=list(scratch))(*args)]
    dot_general x7 -> x0, matrix products: 8.99 us -> none  [the longest x1 2.3 us: local(): jnp.einsum('sach,ahd->sacd', routed_hidden, down_weight, preferred_elemen...]
    concatenate x2 -> x0, local copies, waits for them, and re-layouts: 1.97 us -> none  [hidden_of(): jnp.concatenate([partial_value, jnp.zeros((extra,) + partial_value.shape[...]
    reduce_sum x4 -> x0, other arithmetic: 1.88 us -> none  [the longest x1 1.47 us: summed_on_arrival(): return jnp.sum(tiles.astype(jnp.float32), axis=0)]
    another operation x3 -> x0, local copies, waits for them, and re-layouts: 1.77 us -> none
  transfers between devices with their start and end apart: 2 -> 0, of which waited for: 2 -> 0; matrix products, arithmetic and copies ran while one was open for 2% -> 0% of each run, Pallas kernels for 0% -> 0%
where the time goes in v1:
time: 145 us; the launch traced here: 144 us
  blocking collectives  130 us (90%)
  Pallas kernels  14 us (10%)
    all_to_all x1, blocking collectives, local(): parts = lax.all_to_all(parts, 'dp', 0, 0, tiled=True)  47.6 us
    all_to_all x1, blocking collectives, local(): lax.all_to_all(sent.reshape(sources, SUB, WIDE), 'expert', 0, 0, tiled=True)  35.7 us
    all_to_all x1, blocking collectives, local(): hidden = lax.all_to_all(copies, 'dp', 0, 0, tiled=True)  27.1 us
    all_to_all x1, blocking collectives, local(): lax.all_to_all(results.reshape(sources, SUB, width), 'expert', 0, 0, tile...  19.7 us
    pallas_call x5, Pallas kernels, call(): pl.pallas_call(body, out_shape=outs, scratch_shapes=list(scratch))(*args)  14 us

profile of v1, /device:TPU:1, one launch (start us, length us, event | category | flops | bytes accessed | tf_op | source)
XLA Modules:
  0.0 144.1 jit_solution(3663654716916093973)
XLA Ops:
  0.0 1.9 %shard_map.100 = (bf16[256,256]{1,0:T(8,128)(2,1)}, f32[256,16]{1,0:T(8,128)}) custom-call(s32[8,16]{1,0:T(8,128)} %bitcast.21, f32[8,16]{1,0:T(8,128)} %bitcast.22, bf16[16,224]{1,0:T(8,128)(2,1)} %r_2_.1, bf16[16,224]{1,0:T(8,128)(2,1)} %r_3_.2), custom_call_target="tpu_custom_call" | custom-call | tf_op jit(solution)/shard_map/pallas_call | solution.py:137
  1.9 35.7 %all_to_all.20 = bf16[32,8,256]{2,1,0:T(8,128)(2,1)} all-to-all(bf16[32,8,256]{2,1,0:T(8,128)(2,1)} %bitcast.20), channel_id=1, replica_groups=mesh['dp'=32,'expert'=32] {'expert'}, dimensions={0} | all-to-all | bytes 262144 | tf_op jit(solution)/shard_map/all_to_all | solution.py:170
  37.6 4.4 %shard_map.101 = bf16[32,192,128]{2,1,0:T(8,128)(2,1)} custom-call(bf16[256,256]{1,0:T(8,128)(2,1)} %bitcast.12, bf16[224,2048]{1,0:T(8,128)(2,1)} %bitcast.16, bf16[224,2048]{1,0:T(8,128)(2,1)} %bitcast.17, bf16[224,2048]{1,0:T(8,128)(2,1)} %r_3_.3, bf16[224,2048]{1,0:T(8,128)(2,1)} %r_4_.1), custom_call_target="tpu_custom_call" | custom-call | tf_op jit(solution)/shard_map/pallas_call | solution.py:137
  42.0 47.6 %all_to_all.21.parts = bf16[32,192,128]{2,1,0:T(8,128)(2,1)} all-to-all(bf16[32,192,128]{2,1,0:T(8,128)(2,1)} %shard_map.101), channel_id=1, replica_groups=mesh['dp'=32,'expert'=32] {'dp'}, dimensions={0} | all-to-all | bytes 3145728 | tf_op jit(solution)/shard_map/all_to_all | solution.py:183
  89.6 2.5 %shard_map.102 = bf16[32,96,128]{2,1,0:T(8,128)(2,1)} custom-call(bf16[32,192,128]{2,1,0:T(8,128)(2,1)} %all_to_all.21.parts), custom_call_target="tpu_custom_call" | custom-call | tf_op jit(solution)/shard_map/pallas_call | solution.py:137
  92.2 27.1 %all_to_all.22.r_0_ = bf16[32,96,128]{2,1,0:T(8,128)(2,1)} all-to-all(bf16[32,96,128]{2,1,0:T(8,128)(2,1)} %shard_map.102), channel_id=1, replica_groups=mesh['dp'=32,'expert'=32] {'dp'}, dimensions={0} | all-to-all | bytes 1572864 | tf_op jit(solution)/shard_map/all_to_all | solution.py:185
  119.2 3.4 %shard_map.103 = bf16[256,224]{1,0:T(8,128)(2,1)} custom-call(bf16[32,96,128]{2,1,0:T(8,128)(2,1)} %all_to_all.22.r_0_, bf16[256,256]{1,0:T(8,128)(2,1)} %bitcast.13, bf16[224,2048]{1,0:T(8,128)(2,1)} %bitcast.14, bf16[224,2048]{1,0:T(8,128)(2,1)} %bitcast.15), custom_call_target="tpu_custom_call" | custom-call | tf_op jit(solution)/shard_map/pallas_call | solution.py:137
  122.6 19.7 %all_to_all.23 = bf16[32,8,224]{2,1,0:T(8,128)(2,1)} all-to-all(bf16[32,8,224]{2,1,0:T(8,128)(2,1)} %bitcast.18), channel_id=1, replica_groups=mesh['dp'=32,'expert'=32] {'expert'}, dimensions={0} | all-to-all | bytes 229376 | tf_op jit(solution)/shard_map/all_to_all | solution.py:196
  142.3 1.8 %shard_map.104 = bf16[16,224]{1,0:T(8,128)(2,1)} custom-call(bf16[256,224]{1,0:T(8,128)(2,1)} %bitcast.19, f32[256,16]{1,0:T(8,128)} %get-tuple-element.8.mix), custom_call_target="tpu_custom_call" | custom-call | tf_op jit(solution)/shard_map/pallas_call | solution.py:137

commit v2 on v1

--- a/solution.py
+++ b/solution.py
@@ -9,6 +9,9 @@
 BF16 = jnp.bfloat16
 LANES = 128
 SUB = 8
+EARLY = 1 << 34
+NEAR = 4
+GRANT = 16 << 20
 WIDE = 256
 
 
@@ -28,7 +31,13 @@
     return jnp.where(hit, 1.0, 0.0).astype(BF16)
 
 
-def pack_body(cap, ids, weight, routed_in, shared_in, out, mix, wide_r, wide_s):
+def pack_body(cap, ids_h, weight_h, routed_h, shared_h, out, mix, ids, weight, routed_in, shared_in, wide_r, wide_s, sems):
+    pairs = ((ids_h, ids), (weight_h, weight), (routed_h, routed_in), (shared_h, shared_in))
+    copies = [pltpu.make_async_copy(a, b, sems.at[n]) for n, (a, b) in enumerate(pairs)]
+    for c in copies:
+        c.start()
+    for c in copies:
+        c.wait()
     top, tokens = ids.shape
     experts = out.shape[0] // SUB
     width = routed_in.shape[1]
@@ -80,6 +89,7 @@
     shared = compact[:, width : width + 1] > 0.5
     left[...] = jnp.where(shared, 0.0, compact).astype(BF16)[:, :width]
     right[...] = jnp.where(shared, compact, 0.0).astype(BF16)[:, :width]
+    odd = lax.axis_index("expert") % 2 == 1
     step = 2 * LANES
     for c in range(units // step):
         cols = slice(c * step, (c + 1) * step)
@@ -89,9 +99,18 @@
             for b in range(2):
                 for j in range(2):
                     owner = 2 * (2 * c + b) + j
-                    out[owner, which * half : (which + 1) * half, :] = value[
+                    swapped = owner % NEAR * (out.shape[0] // NEAR) + owner // NEAR
+                    out[jnp.where(odd, swapped, owner), which * half : (which + 1) * half, :] = value[
                         j * half : (j + 1) * half, b * LANES : (b + 1) * LANES
                     ]
+
+
+def add_body(parts, out):
+    for q in range(out.shape[0]):
+        total = parts[0, q].astype(F32)
+        for s in range(1, parts.shape[0]):
+            total = total + parts[s, q].astype(F32)
+        out[q] = total.astype(BF16)
 
 
 def act_body(parts, out):
@@ -103,7 +122,7 @@
         gate = gate + parts[s, :half, :].astype(F32)
         upper = upper + parts[s, half:, :].astype(F32)
     hidden = (jax.nn.silu(gate) * upper).astype(BF16)
-    for s in range(sources):
+    for s in range(out.shape[0]):
         out[s] = hidden
 
 
@@ -131,10 +150,36 @@
     out[...] = value.astype(BF16)
 
 
-def call(body, shape, dtype, *args, scratch=()):
-    single = isinstance(dtype, tuple)
-    outs = [jax.ShapeDtypeStruct(s, d) for s, d in zip(shape, dtype)] if single else jax.ShapeDtypeStruct(shape, dtype)
-    return pl.pallas_call(body, out_shape=outs, scratch_shapes=list(scratch))(*args)
+def call(body, shape, dtype, *args, scratch=(), in_hbm=0, flops=0):
+    several = isinstance(dtype, tuple)
+    outs = [jax.ShapeDtypeStruct(a, d) for a, d in zip(shape, dtype)] if several else jax.ShapeDtypeStruct(shape, dtype)
+    hbm, vmem = pl.BlockSpec(memory_space=pltpu.HBM), pl.BlockSpec(memory_space=pltpu.VMEM)
+    return pl.pallas_call(
+        body,
+        out_shape=outs,
+        in_specs=[hbm if n < in_hbm else vmem for n in range(len(args))],
+        scratch_shapes=list(scratch),
+        compiler_params=pltpu.CompilerParams(vmem_limit_bytes=GRANT),
+        cost_estimate=pl.CostEstimate(flops=flops, bytes_accessed=0, transcendentals=0) if flops else None,
+    )(*[pltpu.with_memory_space_constraint(a, pltpu.HBM) if n < in_hbm else a for n, a in enumerate(args)])
+
+
+def stage_groups(owners, experts):
+    down, across = owners // NEAR, NEAR
+    rank = lambda y, x, e: (y * across + x) * experts + e
+    first, second = [], []
+    for e in range(experts):
+        if e % 2:
+            first += [[rank(y, x, e) for x in range(across)] for y in range(down)]
+            second += [[rank(y, x, e) for y in range(down)] for x in range(across)]
+        else:
+            first += [[rank(2 * i + h, x, e) for i in range(down // 2)] for h in range(2) for x in range(across)]
+            second += [[rank(2 * i + h, x, e) for h in range(2) for x in range(across)] for i in range(down // 2)]
+    return first, second
+
+
+def exchange(array, groups):
+    return lax.all_to_all(array, ("dp", "expert"), 0, 0, tiled=True, axis_index_groups=groups)
 
 
 def local(
@@ -165,7 +210,17 @@
         route_weight.T,
         shortcut_in,
         current_in,
-        scratch=(pltpu.VMEM((tokens, WIDE), BF16), pltpu.VMEM((tokens, WIDE), BF16)),
+        in_hbm=4,
+        flops=EARLY,
+        scratch=(
+            pltpu.VMEM((top, tokens), jnp.int32),
+            pltpu.VMEM((top, tokens), F32),
+            pltpu.VMEM((tokens, width), BF16),
+            pltpu.VMEM((tokens, width), BF16),
+            pltpu.VMEM((tokens, WIDE), BF16),
+            pltpu.VMEM((tokens, WIDE), BF16),
+            pltpu.SemaphoreType.DMA((4,)),
+        ),
     )
     arrived = lax.all_to_all(sent.reshape(sources, SUB, WIDE), "expert", 0, 0, tiled=True)
     arrived = arrived.reshape(padded, WIDE)
@@ -180,7 +235,11 @@
         shared_up,
         scratch=(pltpu.VMEM((rows, width), BF16), pltpu.VMEM((rows, width), BF16)),
     )
-    parts = lax.all_to_all(parts, "dp", 0, 0, tiled=True)
+    first, second = stage_groups(owners, sources)
+    far = owners // NEAR
+    parts = exchange(parts.reshape(NEAR, far * rows, LANES), first)
+    parts = call(add_body, (far, rows, LANES), BF16, parts.reshape(NEAR, far, rows, LANES))
+    parts = exchange(parts, second)
     copies = call(act_body, (owners, rows // 2, LANES), BF16, parts)
     hidden = lax.all_to_all(copies, "dp", 0, 0, tiled=True)
     results = call(

time: 145 us -> 126 us (0.87)
  Pallas kernels: 14 us -> 4.67 us
  blocking collectives: 130 us -> 121 us
    pallas_call x5 -> x6, Pallas kernels: 14 us -> 4.67 us  [call(): pl.pallas_call(body, out_shape=outs, in_specs=[hbm if n < in_hbm else vme...]
    all_to_all x1 -> x2, blocking collectives: 47.6 us -> 43.1 us  [exchange(): lax.all_to_all(array, ('dp', 'expert'), 0, 0, tiled=True, axis_index_grou...]
    all_to_all x1, blocking collectives: 27.1 us -> 24.6 us  [local(): hidden = lax.all_to_all(copies, 'dp', 0, 0, tiled=True)]
    all_to_all x1, blocking collectives: 19.7 us -> 17.5 us  [local(): lax.all_to_all(results.reshape(sources, SUB, width), 'expert', 0, 0, tile...]
where the time goes in v2:
time: 126 us; the launch traced here: 125 us
  blocking collectives  121 us (96%)
  Pallas kernels  4.67 us (4%)
    all_to_all x2, blocking collectives, exchange(): lax.all_to_all(array, ('dp', 'expert'), 0, 0, tiled=True, axis_index_grou...  43.1 us
    all_to_all x1, blocking collectives, local(): lax.all_to_all(sent.reshape(sources, SUB, WIDE), 'expert', 0, 0, tiled=True)  35.4 us
    all_to_all x1, blocking collectives, local(): hidden = lax.all_to_all(copies, 'dp', 0, 0, tiled=True)  24.6 us
    all_to_all x1, blocking collectives, local(): lax.all_to_all(results.reshape(sources, SUB, width), 'expert', 0, 0, tile...  17.5 us
    pallas_call x6, Pallas kernels, call(): pl.pallas_call(body, out_shape=outs, in_specs=[hbm if n < in_hbm else vme...  4.67 us

profile of v2, /device:TPU:1, one launch (start us, length us, event | category | flops | bytes accessed | tf_op | source)
XLA Modules:
  0.0 125.3 jit_solution(18401709747425904188)
XLA Ops:
  0.0 0.0 copy-start.2
  0.0 0.0 copy-start.3
  0.0 0.0 copy-start.4
  0.0 0.0 copy-start.5
  0.0 1.4 %shard_map.100 = (bf16[256,256]{1,0:T(8,128)(2,1)S(1)}, f32[256,16]{1,0:T(8,128)S(1)}) custom-call(s32[8,16]{1,0:T(8,128)} %bitcast.25, f32[8,16]{1,0:T(8,128)} %bitcast.26, bf16[16,224]{1,0:T(8,128)(2,1)} %r_2_.1, bf16[16,224]{1,0:T(8,128)(2,1)} %r_3_.2), custom_call_target="tpu_custom_call" | custom-call | flops 17179869184 | tf_op jit(solution)/shard_map/pallas_call | solution.py:157
  1.4 35.4 %all_to_all.25 = bf16[32,8,256]{2,1,0:T(8,128)(2,1)S(1)} all-to-all(bf16[32,8,256]{2,1,0:T(8,128)(2,1)S(1)} %bitcast.24), channel_id=1, replica_groups=mesh['dp'=32,'expert'=32] {'expert'}, dimensions={0} | all-to-all | bytes 262144 | tf_op jit(solution)/shard_map/all_to_all | solution.py:225
  36.8 0.0 copy-done.2
  36.8 0.0 copy-done.3
  36.8 0.0 copy-done.4
  36.8 0.0 copy-done.5
  36.8 1.2 shard_map.101
  38.1 23.6 %all_to_all.26 = bf16[4,1536,128]{2,1,0:T(8,128)(2,1)S(1)} all-to-all(bf16[4,1536,128]{2,1,0:T(8,128)(2,1)S(1)} %bitcast.15), channel_id=1, replica_groups={{0,256,512,768},{32,288,544,800},{64,320,576,832},{96,352,608,864},{128..., dimensions={0} | all-to-all | bytes 3145728 | tf_op jit(solution)/shard_map/all_to_all | solution.py:182
  61.6 0.2 shard_map.102
  61.8 19.6 %all_to_all.27.parts = bf16[8,192,128]{2,1,0:T(8,128)(2,1)S(1)} all-to-all(bf16[8,192,128]{2,1,0:T(8,128)(2,1)S(1)} %shard_map.102), channel_id=1, replica_groups={{0,32,64,96,128,160,192,224},{256,288,320,352,384,416,448,480},{512,544..., dimensions={0} | all-to-all | bytes 786432 | tf_op jit(solution)/shard_map/all_to_all | solution.py:182
  81.4 0.0 copy-start
  81.4 0.0 copy-start.1
  81.4 0.1 shard_map.103
  81.5 24.6 %all_to_all.28.r_0_ = bf16[32,96,128]{2,1,0:T(8,128)(2,1)S(1)} all-to-all(bf16[32,96,128]{2,1,0:T(8,128)(2,1)S(1)} %shard_map.103), channel_id=1, replica_groups=mesh['dp'=32,'expert'=32] {'dp'}, dimensions={0} | all-to-all | bytes 1572864 | tf_op jit(solution)/shard_map/all_to_all | solution.py:244
  106.0 0.0 copy-done
  106.0 0.0 copy-done.1
  106.0 0.9 shard_map.104
  107.0 17.5 %all_to_all.29 = bf16[32,8,224]{2,1,0:T(8,128)(2,1)S(1)} all-to-all(bf16[32,8,224]{2,1,0:T(8,128)(2,1)S(1)} %bitcast.22), channel_id=1, replica_groups=mesh['dp'=32,'expert'=32] {'expert'}, dimensions={0} | all-to-all | bytes 229376 | tf_op jit(solution)/shard_map/all_to_all | solution.py:255
  124.5 0.9 shard_map.105
Async XLA Ops:
  0.0 36.8 %copy-start.2 = (bf16[1,224,2048]{2,1,0:T(8,128)(2,1)S(1)}, bf16[1,224,2048]{2,1,0:T(8,128)(2,1)}, u32[]{:S(2)}) copy-start(bf16[1,224,2048]{2,1,0:T(8,128)(2,1)} %param.14) | copy-start | bytes 2752516
  0.0 36.8 %copy-start.3 = (bf16[1,224,2048]{2,1,0:T(8,128)(2,1)S(1)}, bf16[1,224,2048]{2,1,0:T(8,128)(2,1)}, u32[]{:S(2)}) copy-start(bf16[1,224,2048]{2,1,0:T(8,128)(2,1)} %param.15) | copy-start | bytes 2752516
  0.0 36.8 %copy-start.4 = (bf16[224,2048]{1,0:T(8,128)(2,1)S(1)}, bf16[224,2048]{1,0:T(8,128)(2,1)}, u32[]{:S(2)}) copy-start(bf16[224,2048]{1,0:T(8,128)(2,1)} %r_3_.3) | copy-start | bytes 2752516
  0.0 36.8 %copy-start.5 = (bf16[224,2048]{1,0:T(8,128)(2,1)S(1)}, bf16[224,2048]{1,0:T(8,128)(2,1)}, u32[]{:S(2)}) copy-start(bf16[224,2048]{1,0:T(8,128)(2,1)} %r_4_.1) | copy-start | bytes 2752516
  81.4 24.7 %copy-start = (bf16[1,2048,224]{1,2,0:T(8,128)(2,1)S(1)}, bf16[1,2048,224]{1,2,0:T(8,128)(2,1)}, u32[]{:S(2)}) copy-start(bf16[1,2048,224]{1,2,0:T(8,128)(2,1)} %param.16) | copy-start | bytes 2752516
  81.4 24.7 %copy-start.1 = (bf16[2048,224]{0,1:T(8,128)(2,1)S(1)}, bf16[2048,224]{0,1:T(8,128)(2,1)}, u32[]{:S(2)}) copy-start(bf16[2048,224]{0,1:T(8,128)(2,1)} %param.19) | copy-start | bytes 2752516

commit v3 on v2

--- a/solution.py
+++ b/solution.py
@@ -10,6 +10,7 @@
 LANES = 128
 SUB = 8
 EARLY = 1 << 34
+RING = ((0, 1, 3, 6), (7, 2, 4, 5))
 NEAR = 4
 GRANT = 16 << 20
 WIDE = 256
@@ -80,7 +81,7 @@
     out[...] = sent.astype(BF16)
 
 
-def up_body(cap, arrived, gate_w, up_w, shared_gate, shared_up, out, left, right):
+def up_body(cap, chunks, arrived, gate_w, up_w, shared_gate, shared_up, out, left, right):
     padded, wide = arrived.shape
     width, units = gate_w.shape
     rows = padded // SUB * cap
@@ -99,8 +100,7 @@
             for b in range(2):
                 for j in range(2):
                     owner = 2 * (2 * c + b) + j
-                    swapped = owner % NEAR * (out.shape[0] // NEAR) + owner // NEAR
-                    out[jnp.where(odd, swapped, owner), which * half : (which + 1) * half, :] = value[
+                    out[jnp.where(odd, chunks[1][owner], chunks[0][owner]), which * half : (which + 1) * half, :] = value[
                         j * half : (j + 1) * half, b * LANES : (b + 1) * LANES
                     ]
 
@@ -166,16 +166,24 @@
 
 def stage_groups(owners, experts):
     down, across = owners // NEAR, NEAR
-    rank = lambda y, x, e: (y * across + x) * experts + e
-    first, second = [], []
+    assert down == 2 * NEAR and across == NEAR
+    stages = ([], [])
+    chunks = [[0] * owners, [0] * owners]
     for e in range(experts):
-        if e % 2:
-            first += [[rank(y, x, e) for x in range(across)] for y in range(down)]
-            second += [[rank(y, x, e) for y in range(down)] for x in range(across)]
+        if e % 2 == 0:
+            one = [[(y, x) for x in range(across)] for y in range(down)]
+            two = [[(y, x) for y in range(down)] for x in range(across)]
         else:
-            first += [[rank(2 * i + h, x, e) for i in range(down // 2)] for h in range(2) for x in range(across)]
-            second += [[rank(2 * i + h, x, e) for h in range(2) for x in range(across)] for i in range(down // 2)]
-    return first, second
+            one = [[(y, x) for y in line] for line in RING for x in range(across)]
+            two = [[(y, x) for y in pair for x in range(across)] for pair in zip(*RING)]
+        place = [{d: group.index(d) for group in stage for d in group} for stage in (one, two)]
+        for y in range(down):
+            for x in range(across):
+                a, b = (p[y, x] for p in place)
+                chunks[e % 2][y * across + x] = a * down + b
+        for groups, stage in zip(stages, (one, two)):
+            groups += [[(y * across + x) * experts + e for y, x in group] for group in stage]
+    return stages, chunks
 
 
 def exchange(array, groups):
@@ -224,8 +232,9 @@
     )
     arrived = lax.all_to_all(sent.reshape(sources, SUB, WIDE), "expert", 0, 0, tiled=True)
     arrived = arrived.reshape(padded, WIDE)
+    (one, two), chunks = stage_groups(owners, sources)
     parts = call(
-        lambda *r: up_body(cap, *r),
+        lambda *r: up_body(cap, chunks, *r),
         (owners, rows, LANES),
         BF16,
         arrived,
@@ -235,11 +244,10 @@
         shared_up,
         scratch=(pltpu.VMEM((rows, width), BF16), pltpu.VMEM((rows, width), BF16)),
     )
-    first, second = stage_groups(owners, sources)
-    far = owners // NEAR
-    parts = exchange(parts.reshape(NEAR, far * rows, LANES), first)
-    parts = call(add_body, (far, rows, LANES), BF16, parts.reshape(NEAR, far, rows, LANES))
-    parts = exchange(parts, second)
+    left = owners // NEAR
+    parts = exchange(parts.reshape(NEAR, left * rows, LANES), one)
+    parts = call(add_body, (left, rows, LANES), BF16, parts.reshape(NEAR, left, rows, LANES))
+    parts = exchange(parts, two)
     copies = call(act_body, (owners, rows // 2, LANES), BF16, parts)
     hidden = lax.all_to_all(copies, "dp", 0, 0, tiled=True)
     results = call(

time: 126 us -> 124 us (0.984)
  blocking collectives: 121 us -> 119 us
    all_to_all x2, blocking collectives: 43.1 us -> 40.3 us  [exchange(): lax.all_to_all(array, ('dp', 'expert'), 0, 0, tiled=True, axis_index_grou...]
where the time goes in v3:
time: 124 us; the launch traced here: 123 us
  blocking collectives  119 us (96%)
  Pallas kernels  4.66 us (4%)
    all_to_all x2, blocking collectives, exchange(): lax.all_to_all(array, ('dp', 'expert'), 0, 0, tiled=True, axis_index_grou...  40.3 us
    all_to_all x1, blocking collectives, local(): lax.all_to_all(sent.reshape(sources, SUB, WIDE), 'expert', 0, 0, tiled=True)  35.4 us
    all_to_all x1, blocking collectives, local(): hidden = lax.all_to_all(copies, 'dp', 0, 0, tiled=True)  25.4 us
    all_to_all x1, blocking collectives, local(): lax.all_to_all(results.reshape(sources, SUB, width), 'expert', 0, 0, tile...  17.5 us
    pallas_call x6, Pallas kernels, call(): pl.pallas_call(body, out_shape=outs, in_specs=[hbm if n < in_hbm else vme...  4.66 us

profile of v3, /device:TPU:1, one launch (start us, length us, event | category | flops | bytes accessed | tf_op | source)
XLA Modules:
  0.0 123.3 jit_solution(9652747950354955337)
XLA Ops:
  0.0 0.0 copy-start.2
  0.0 0.0 copy-start.3
  0.0 0.0 copy-start.4
  0.0 0.0 copy-start.5
  0.0 1.4 %shard_map.100 = (bf16[256,256]{1,0:T(8,128)(2,1)S(1)}, f32[256,16]{1,0:T(8,128)S(1)}) custom-call(s32[8,16]{1,0:T(8,128)} %bitcast.25, f32[8,16]{1,0:T(8,128)} %bitcast.26, bf16[16,224]{1,0:T(8,128)(2,1)} %r_2_.1, bf16[16,224]{1,0:T(8,128)(2,1)} %r_3_.2), custom_call_target="tpu_custom_call" | custom-call | flops 17179869184 | tf_op jit(solution)/shard_map/pallas_call | solution.py:157
  1.4 35.4 %all_to_all.25 = bf16[32,8,256]{2,1,0:T(8,128)(2,1)S(1)} all-to-all(bf16[32,8,256]{2,1,0:T(8,128)(2,1)S(1)} %bitcast.24), channel_id=1, replica_groups=mesh['dp'=32,'expert'=32] {'expert'}, dimensions={0} | all-to-all | bytes 262144 | tf_op jit(solution)/shard_map/all_to_all | solution.py:233
  36.8 0.0 copy-done.2
  36.8 0.0 copy-done.3
  36.8 0.0 copy-done.4
  36.8 0.0 copy-done.5
  36.8 1.2 shard_map.101
  38.1 26.7 %all_to_all.26 = bf16[4,1536,128]{2,1,0:T(8,128)(2,1)S(1)} all-to-all(bf16[4,1536,128]{2,1,0:T(8,128)(2,1)S(1)} %bitcast.15), channel_id=1, replica_groups={{0,32,64,96},{128,160,192,224},{256,288,320,352},{384,416,448,480},{512..., dimensions={0} | all-to-all | bytes 3145728 | tf_op jit(solution)/shard_map/all_to_all | solution.py:190
  64.8 0.2 shard_map.102
  65.0 13.6 %all_to_all.27.parts = bf16[8,192,128]{2,1,0:T(8,128)(2,1)S(1)} all-to-all(bf16[8,192,128]{2,1,0:T(8,128)(2,1)S(1)} %shard_map.102), channel_id=1, replica_groups={{0,128,256,384,512,640,768,896},{32,160,288,416,544,672,800,928},{64,19..., dimensions={0} | all-to-all | bytes 786432 | tf_op jit(solution)/shard_map/all_to_all | solution.py:190
  78.5 0.0 copy-start
  78.5 0.0 copy-start.1
  78.5 0.1 shard_map.103
  78.6 25.4 %all_to_all.28.r_0_ = bf16[32,96,128]{2,1,0:T(8,128)(2,1)S(1)} all-to-all(bf16[32,96,128]{2,1,0:T(8,128)(2,1)S(1)} %shard_map.103), channel_id=1, replica_groups=mesh['dp'=32,'expert'=32] {'dp'}, dimensions={0} | all-to-all | bytes 1572864 | tf_op jit(solution)/shard_map/all_to_all | solution.py:252
  104.0 0.0 copy-done
  104.0 0.0 copy-done.1
  104.0 0.9 shard_map.104
  105.0 17.5 %all_to_all.29 = bf16[32,8,224]{2,1,0:T(8,128)(2,1)S(1)} all-to-all(bf16[32,8,224]{2,1,0:T(8,128)(2,1)S(1)} %bitcast.22), channel_id=1, replica_groups=mesh['dp'=32,'expert'=32] {'expert'}, dimensions={0} | all-to-all | bytes 229376 | tf_op jit(solution)/shard_map/all_to_all | solution.py:263
  122.4 0.9 shard_map.105
Async XLA Ops:
  0.0 36.8 %copy-start.2 = (bf16[1,224,2048]{2,1,0:T(8,128)(2,1)S(1)}, bf16[1,224,2048]{2,1,0:T(8,128)(2,1)}, u32[]{:S(2)}) copy-start(bf16[1,224,2048]{2,1,0:T(8,128)(2,1)} %param.14) | copy-start | bytes 2752516
  0.0 36.8 %copy-start.3 = (bf16[1,224,2048]{2,1,0:T(8,128)(2,1)S(1)}, bf16[1,224,2048]{2,1,0:T(8,128)(2,1)}, u32[]{:S(2)}) copy-start(bf16[1,224,2048]{2,1,0:T(8,128)(2,1)} %param.15) | copy-start | bytes 2752516
  0.0 36.8 %copy-start.4 = (bf16[224,2048]{1,0:T(8,128)(2,1)S(1)}, bf16[224,2048]{1,0:T(8,128)(2,1)}, u32[]{:S(2)}) copy-start(bf16[224,2048]{1,0:T(8,128)(2,1)} %r_3_.3) | copy-start | bytes 2752516
  0.0 36.8 %copy-start.5 = (bf16[224,2048]{1,0:T(8,128)(2,1)S(1)}, bf16[224,2048]{1,0:T(8,128)(2,1)}, u32[]{:S(2)}) copy-start(bf16[224,2048]{1,0:T(8,128)(2,1)} %r_4_.1) | copy-start | bytes 2752516
  78.5 25.5 %copy-start = (bf16[1,2048,224]{1,2,0:T(8,128)(2,1)S(1)}, bf16[1,2048,224]{1,2,0:T(8,128)(2,1)}, u32[]{:S(2)}) copy-start(bf16[1,2048,224]{1,2,0:T(8,128)(2,1)} %param.16) | copy-start | bytes 2752516
  78.5 25.5 %copy-start.1 = (bf16[2048,224]{0,1:T(8,128)(2,1)S(1)}, bf16[2048,224]{0,1:T(8,128)(2,1)}, u32[]{:S(2)}) copy-start(bf16[2048,224]{0,1:T(8,128)(2,1)} %param.19) | copy-start | bytes 2752516

commit v4 on v3

--- a/solution.py
+++ b/solution.py
@@ -81,13 +81,14 @@
     out[...] = sent.astype(BF16)
 
 
-def up_body(cap, chunks, arrived, gate_w, up_w, shared_gate, shared_up, out, left, right):
+def up_body(cap, chunks, arrived, gate_w, up_w, shared_gate, shared_up, out, flags, left, right):
     padded, wide = arrived.shape
     width, units = gate_w.shape
     rows = padded // SUB * cap
     half = rows // 2
     compact = dot(pick_rows(rows, padded, cap), arrived[...])
     shared = compact[:, width : width + 1] > 0.5
+    flags[...] = jnp.broadcast_to(jnp.where(shared, 1.0, 0.0), flags.shape)
     left[...] = jnp.where(shared, 0.0, compact).astype(BF16)[:, :width]
     right[...] = jnp.where(shared, compact, 0.0).astype(BF16)[:, :width]
     odd = lax.axis_index("expert") % 2 == 1
@@ -126,23 +127,18 @@
         out[s] = hidden
 
 
-def down_body(cap, hidden, arrived, down_t, shared_down_t, out, joined):
+def down_body(cap, hidden, flags, down_t, shared_down_t, out, joined):
     owners, half, _ = hidden.shape
-    padded = arrived.shape[0]
-    width = down_t.shape[0]
+    padded = out.shape[0]
     rows = 2 * half
     for owner in range(owners):
         i, j = owner // 2, owner % 2
         joined[j * half : (j + 1) * half, i * LANES : (i + 1) * LANES] = hidden[owner]
     last = ((1,), (1,))
-    own = dot(joined[...], down_t[...], last).astype(BF16)
-    common = dot(joined[...], shared_down_t[...], last).astype(BF16)
-    back = pick_rows(rows, padded, cap)
-    first = ((0,), (0,))
-    own = dot(back, own, first)
-    common = dot(back, common, first)
-    shared = arrived[:, width:].astype(F32)[:, :1] > 0.5
-    out[...] = jnp.where(shared, common, own).astype(BF16)
+    own = dot(joined[...], down_t[...], last)
+    common = dot(joined[...], shared_down_t[...], last)
+    value = jnp.where(flags[:, :1] > 0.5, common, own).astype(BF16)
+    out[...] = dot(pick_rows(rows, padded, cap), value, ((0,), (0,))).astype(BF16)
 
 
 def mix_body(returned, mix, out):
@@ -233,10 +229,10 @@
     arrived = lax.all_to_all(sent.reshape(sources, SUB, WIDE), "expert", 0, 0, tiled=True)
     arrived = arrived.reshape(padded, WIDE)
     (one, two), chunks = stage_groups(owners, sources)
-    parts = call(
+    parts, flags = call(
         lambda *r: up_body(cap, chunks, *r),
-        (owners, rows, LANES),
-        BF16,
+        ((owners, rows, LANES), (rows, LANES)),
+        (BF16, F32),
         arrived,
         gate_weight[0],
         up_weight[0],
@@ -255,7 +251,7 @@
         (padded, width),
         BF16,
         hidden,
-        arrived,
+        flags,
         down_weight[0].T,
         shared_down.T,
         scratch=(pltpu.VMEM((rows, units), BF16),),

time: 124 us -> 124 us (level)
  no operation moved by 1% of the time
where the time goes in v4:
time: 124 us; the launch traced here: 123 us
  blocking collectives  119 us (96%)
  Pallas kernels  4.63 us (4%)
    all_to_all x2, blocking collectives, exchange(): lax.all_to_all(array, ('dp', 'expert'), 0, 0, tiled=True, axis_index_grou...  40.3 us
    all_to_all x1, blocking collectives, local(): lax.all_to_all(sent.reshape(sources, SUB, WIDE), 'expert', 0, 0, tiled=True)  35.4 us
    all_to_all x1, blocking collectives, local(): hidden = lax.all_to_all(copies, 'dp', 0, 0, tiled=True)  25.4 us
    all_to_all x1, blocking collectives, local(): lax.all_to_all(results.reshape(sources, SUB, width), 'expert', 0, 0, tile...  17.5 us
    pallas_call x6, Pallas kernels, call(): pl.pallas_call(body, out_shape=outs, in_specs=[hbm if n < in_hbm else vme...  4.63 us

profile of v4, /device:TPU:1, one launch (start us, length us, event | category | flops | bytes accessed | tf_op | source)
XLA Modules:
  0.0 123.3 jit_solution(12537503439273865703)
XLA Ops:
  0.0 0.0 copy-start.2
  0.0 0.0 copy-start.3
  0.0 0.0 copy-start.4
  0.0 0.0 copy-start.5
  0.0 1.4 %shard_map.100 = (bf16[256,256]{1,0:T(8,128)(2,1)S(1)}, f32[256,16]{1,0:T(8,128)S(1)}) custom-call(s32[8,16]{1,0:T(8,128)} %bitcast.24, f32[8,16]{1,0:T(8,128)} %bitcast.25, bf16[16,224]{1,0:T(8,128)(2,1)} %r_2_.1, bf16[16,224]{1,0:T(8,128)(2,1)} %r_3_.2), custom_call_target="tpu_custom_call" | custom-call | flops 17179869184 | tf_op jit(solution)/shard_map/pallas_call | solution.py:153
  1.4 35.4 %all_to_all.25 = bf16[32,8,256]{2,1,0:T(8,128)(2,1)S(1)} all-to-all(bf16[32,8,256]{2,1,0:T(8,128)(2,1)S(1)} %bitcast.23), channel_id=1, replica_groups=mesh['dp'=32,'expert'=32] {'expert'}, dimensions={0} | all-to-all | bytes 262144 | tf_op jit(solution)/shard_map/all_to_all | solution.py:229
  36.8 0.0 copy-done.2
  36.8 0.0 copy-done.3
  36.8 0.0 copy-done.4
  36.8 0.0 copy-done.5
  36.8 1.2 shard_map.101
  38.1 26.7 %all_to_all.26 = bf16[4,1536,128]{2,1,0:T(8,128)(2,1)S(1)} all-to-all(bf16[4,1536,128]{2,1,0:T(8,128)(2,1)S(1)} %bitcast.15), channel_id=1, replica_groups={{0,32,64,96},{128,160,192,224},{256,288,320,352},{384,416,448,480},{512..., dimensions={0} | all-to-all | bytes 3145728 | tf_op jit(solution)/shard_map/all_to_all | solution.py:186
  64.8 0.2 shard_map.102
  65.0 13.6 %all_to_all.27.parts = bf16[8,192,128]{2,1,0:T(8,128)(2,1)S(1)} all-to-all(bf16[8,192,128]{2,1,0:T(8,128)(2,1)S(1)} %shard_map.102), channel_id=1, replica_groups={{0,128,256,384,512,640,768,896},{32,160,288,416,544,672,800,928},{64,19..., dimensions={0} | all-to-all | bytes 786432 | tf_op jit(solution)/shard_map/all_to_all | solution.py:186
  78.5 0.0 copy-start
  78.5 0.0 copy-start.1
  78.5 0.1 shard_map.103
  78.6 25.4 %all_to_all.28.r_0_ = bf16[32,96,128]{2,1,0:T(8,128)(2,1)S(1)} all-to-all(bf16[32,96,128]{2,1,0:T(8,128)(2,1)S(1)} %shard_map.103), channel_id=1, replica_groups=mesh['dp'=32,'expert'=32] {'dp'}, dimensions={0} | all-to-all | bytes 1572864 | tf_op jit(solution)/shard_map/all_to_all | solution.py:248
  104.0 0.0 copy-done
  104.0 0.0 copy-done.1
  104.0 0.9 shard_map.104
  104.9 17.5 %all_to_all.29 = bf16[32,8,224]{2,1,0:T(8,128)(2,1)S(1)} all-to-all(bf16[32,8,224]{2,1,0:T(8,128)(2,1)S(1)} %bitcast.20), channel_id=1, replica_groups=mesh['dp'=32,'expert'=32] {'expert'}, dimensions={0} | all-to-all | bytes 229376 | tf_op jit(solution)/shard_map/all_to_all | solution.py:259
  122.4 0.9 shard_map.105
Async XLA Ops:
  0.0 36.8 %copy-start.2 = (bf16[1,224,2048]{2,1,0:T(8,128)(2,1)S(1)}, bf16[1,224,2048]{2,1,0:T(8,128)(2,1)}, u32[]{:S(2)}) copy-start(bf16[1,224,2048]{2,1,0:T(8,128)(2,1)} %param.14) | copy-start | bytes 2752516
  0.0 36.8 %copy-start.3 = (bf16[1,224,2048]{2,1,0:T(8,128)(2,1)S(1)}, bf16[1,224,2048]{2,1,0:T(8,128)(2,1)}, u32[]{:S(2)}) copy-start(bf16[1,224,2048]{2,1,0:T(8,128)(2,1)} %param.15) | copy-start | bytes 2752516
  0.0 36.8 %copy-start.4 = (bf16[224,2048]{1,0:T(8,128)(2,1)S(1)}, bf16[224,2048]{1,0:T(8,128)(2,1)}, u32[]{:S(2)}) copy-start(bf16[224,2048]{1,0:T(8,128)(2,1)} %r_3_.3) | copy-start | bytes 2752516
  0.0 36.8 %copy-start.5 = (bf16[224,2048]{1,0:T(8,128)(2,1)S(1)}, bf16[224,2048]{1,0:T(8,128)(2,1)}, u32[]{:S(2)}) copy-start(bf16[224,2048]{1,0:T(8,128)(2,1)} %r_4_.1) | copy-start | bytes 2752516
  78.5 25.5 %copy-start = (bf16[1,2048,224]{1,2,0:T(8,128)(2,1)S(1)}, bf16[1,2048,224]{1,2,0:T(8,128)(2,1)}, u32[]{:S(2)}) copy-start(bf16[1,2048,224]{1,2,0:T(8,128)(2,1)} %param.16) | copy-start | bytes 2752516
  78.5 25.5 %copy-start.1 = (bf16[2048,224]{0,1:T(8,128)(2,1)S(1)}, bf16[2048,224]{0,1:T(8,128)(2,1)}, u32[]{:S(2)}) copy-start(bf16[2048,224]{0,1:T(8,128)(2,1)} %param.19) | copy-start | bytes 2752516
